TPU v7x, 32 devices: a whole 2x2x4 slice. The times are simulated.
32 devices in a mesh: elem: 16 (over z, y, x), param: 2 (over core).
Axes of the slice: x: 2, y: 2, z: 4, core: 2. Of those that a mesh axis runs over, the one named last changes fastest.
Arguments:
- coords: bfloat16 [8, 300], P('param'), may hold values from -6 to 6
- basis_rows: bfloat16 [3, 300, 4096], P(None, None, 'elem'), may hold values from -0.375 to 0.375
- connectivity: int32 [4096, 8], P(('elem', 'param')), may hold values from 0 to 319, as said below
- modulus: float32 [4096], P(('elem', 'param')), may hold values from 0.5 to 15
- stiffness: float32 [24, 24], replicated, may hold values from -1.25 to 1.25
Outputs:
- training: bfloat16 [8, 300, 4096], P(None, None, ('elem', 'param'))
- target: float32 [8, 300], replicated
Inputs may be any that keep to these rules, and one draw needn't show every extreme that they name: `connectivity`: A number c of 256 or more names node c - 256 of the next node block; the last block's next block is the first. An element's eight corner numbers lie among min(8, 64) consecutive numbers; where these lie in the block is not tied to the element's position.
All inputs are finite; a program needn't handle non-finite values.
Results may differ from a plain program's by a relative error of at most 0.0072.
Values may be sent and summed in bfloat16 or wider, within the bound.
A program may use at most 64 MiB of HBM per device.

v0:
```python
import math
import jax
import jax.numpy as jnp
from jax import lax
from jax.sharding import PartitionSpec as P


def passed_along(value, axis, by):
    peers = lax.axis_size(axis)
    return lax.ppermute(value, axis, [(i, (i + by) % peers) for i in range(peers)])


def local(coords, basis_rows, connectivity, modulus, stiffness):
    node_count = basis_rows.shape[2]
    ghost_count = node_count // 4
    ghost_rows = passed_along(basis_rows[:, :, :ghost_count], "elem", -1)
    extended = jnp.concatenate([basis_rows, ghost_rows], axis=2)
    corner_ids = connectivity.T
    elem_count = corner_ids.shape[1]
    element_basis = extended[:, :, corner_ids]
    cycle_size = lax.axis_size("param")
    all_coords = lax.all_gather(coords, "param", axis=0, tiled=True)
    displaced = jnp.stack(
        [
            jnp.dot(all_coords, extended[component], preferred_element_type=jnp.float32)
            for component in range(3)
        ],
        axis=1,
    ).astype(jnp.bfloat16)
    snaps = displaced.shape[0]
    corner_disp = displaced[:, :, corner_ids].reshape(snaps, 24, elem_count).astype(jnp.float32)
    linear = jnp.einsum("kj,sje->ske", stiffness, corner_disp, precision=lax.Precision.HIGHEST)
    forces = (modulus * (linear + 0.25 * corner_disp * corner_disp * corner_disp)).astype(
        jnp.bfloat16
    )
    forces = forces.reshape(snaps, 3, 8, elem_count)
    matrix = jnp.einsum("cmae,scae->sme", element_basis, forces, preferred_element_type=jnp.float32)
    norm_sums = jnp.sum(jnp.sqrt(jnp.sum(matrix * matrix, axis=1)), axis=1)
    force_sums = jnp.sum(matrix, axis=2)
    norm_sums, force_sums = lax.psum((norm_sums, force_sums), ("elem", "param"))
    elem_total = elem_count * lax.axis_size("elem") * cycle_size
    row_scale = norm_sums / elem_total
    target = force_sums / (row_scale[:, None] * math.sqrt(elem_total))
    training = (matrix / row_scale[:, None, None]).astype(jnp.bfloat16)
    return (training, target)


def solution(mesh):
    in_specs = (
        P("param", None),
        P(None, None, "elem"),
        P(("elem", "param"), None),
        P(("elem", "param")),
        P(),
    )
    out_specs = (P(None, None, ("elem", "param")), P())
    return jax.shard_map(local, mesh=mesh, in_specs=in_specs, out_specs=out_specs, check_vma=False)
```

profile of v0, /device:TPU:0, one launch (start us, length us, event | category | flops | bytes accessed | tf_op | source)
XLA Modules:
  0.0 81.1 jit_solution(3763947510035681350)
XLA Ops:
  0.6 1.5 %copy.29 = bf16[3,300,256]{1,0,2:T(4,128)(2,1)S(1)} copy(bf16[3,300,256]{2,1,0:T(8,128)(2,1)} %param.6) | data formatting | bytes 921600 | tf_op args[1]
  2.2 7.0 %collective-permute-start = (bf16[3,300,64]{1,0,2:T(4,128)(2,1)S(1)}, bf16[3,300,64]{1,0,2:T(4,128)(2,1)S(1)}, u32[]{:S(2)}, u32[]{:S(2)}) collective-permute-start(bf16[3,300,64]{1,0,2:T(4,128)(2,1)S(1)} %slice.20), channel_id=1, source_target_pairs={{0,30},{2,0},{4,2},{6,4},{8,6},{10,8},{12,10},{14,12},{16,14},{18,... | collective-permute-start | bytes 345608 | tf_op jit(solution)/shard_map/ppermute | solution.py:10
  9.2 1.9 %all-gather = bf16[2,4,300]{2,1,0:T(4,128)(2,1)S(1)} all-gather(bf16[1,4,300]{2,1,0:T(4,128)(2,1)} %bitcast.72), channel_id=1, replica_groups=mesh['elem'=16,'param'=2] {'param'}, dimensions={0}, use_global_device_ids=true | all-gather | bytes 7200 | tf_op jit(solution)/shard_map/all_gather | solution.py:22
  11.2 0.7 fusion.21
  11.9 1.5 %collective-permute-done = bf16[3,300,64]{1,0,2:T(4,128)(2,1)S(1)} collective-permute-done((bf16[3,300,64]{1,0,2:T(4,128)(2,1)S(1)}, bf16[3,300,64]{1,0,2:T(4,128)(2,1)S(1)}, u32[]{:S(2)}, u32[]{:S(2)}) %collective-permute-start) | collective-permute-done | bytes 115232 | tf_op jit(solution)/shard_map/ppermute | solution.py:10
  13.4 2.1 %fusion.12 = (bf16[1,300,320]{1,0,2:T(2,128)(2,1)S(1)}, bf16[1,300,320]{1,0,2:T(2,128)(2,1)S(1)}, bf16[1,300,320]{1,0,2:T(2,128)(2,1)S(1)}) fusion(bf16[3,300,256]{1,0,2:T(4,128)(2,1)S(1)} %copy.29, bf16[3,300,64]{1,0,2:T(4,128)(2,1)S(1)} %collective-permute-done), kind=kLoop, calls=%fused_computation.28 | loop fusion | flops 288000 | bytes 1152000 | tf_op jit(solution)/shard_map/concatenate | solution.py:17
  15.5 0.9 %copy.30 = bf16[1,300,320]{2,1,0:T(8,128)(2,1)S(1)} copy(bf16[1,300,320]{1,0,2:T(2,128)(2,1)S(1)} %get-tuple-element.14) | data formatting | bytes 384000 | tf_op jit(solution)/shard_map/slice | solution.py:25
  16.3 0.9 %copy.31 = bf16[1,300,320]{2,1,0:T(8,128)(2,1)S(1)} copy(bf16[1,300,320]{1,0,2:T(2,128)(2,1)S(1)} %get-tuple-element.15) | data formatting | bytes 384000 | tf_op jit(solution)/shard_map/slice | solution.py:25
  17.2 0.1 fusion.9
  17.4 0.2 fusion.10
  17.5 0.9 %copy.32 = bf16[1,300,320]{2,1,0:T(8,128)(2,1)S(1)} copy(bf16[1,300,320]{1,0,2:T(2,128)(2,1)S(1)} %get-tuple-element.16) | data formatting | bytes 384000 | tf_op jit(solution)/shard_map/slice | solution.py:25
  18.4 0.1 fusion.11
  18.5 0.2 copy.33
  18.8 3.6 %gather_fusion = bf16[1024,8,3]{1,2,0:T(4,128)(2,1)S(1)} fusion(bf16[8,3,320]{0,1,2:T(4,128)(2,1)S(1)} %copy.33, s32[1024]{0:T(1024)S(1)} %fusion.21), kind=kCustom, calls=%fused_computation | custom fusion | bytes 102400 | tf_op jit(solution)/shard_map/gather | solution.py:31
  22.3 0.5 copy.34
  22.9 0.2 fusion.8
  23.0 0.4 copy.36
  23.5 0.7 pad_maximum_fusion
  24.1 9.9 %gather_fusion.1 = bf16[1024,3,300]{2,1,0:T(4,128)(2,1)} fusion(bf16[3,300,320]{1,0,2:T(4,128)(2,1)S(1)} %pad_maximum_fusion, s32[1024]{0:T(1024)S(1)} %fusion.21), kind=kCustom, calls=%fused_computation.1 | custom fusion | bytes 3690496 | tf_op jit(solution)/shard_map/gather | solution.py:20
  34.1 4.0 %bitcast_reduce_fusion = (f32[8,300]{1,0:T(8,128)S(1)}, f32[8,128]{0,1:T(8,128)S(1)}, f32[128,8,300,1]{2,1,3,0:T(8,128)S(1)}) fusion(bf16[8,3,8,128]{2,0,1,3:T(8,128)(2,1)S(1)} %copy.36, bf16[8,128,3,300]{3,2,1,0:T(4,128)(2,1)} %bitcast.71), kind=kOutput, calls=%fused_computation.5 | convolution fusion | flops 15663776 | bytes 3134848 | tf_op jit(solution)/shard_map/cmae,scae->sme/dot_general | solution.py:37
  38.1 40.7 %all-reduce = (f32[8]{0:T(128)S(1)}, f32[8,300]{1,0:T(8,128)S(1)}) all-reduce(f32[8]{0:T(128)S(1)} %sqrt_reduce_fusion, f32[8,300]{1,0:T(8,128)S(1)} %get-tuple-element.10), channel_id=1, replica_groups=mesh['elem'=16,'param'=2] {'elem','param'}, use_global_device_ids=true, to_apply=%region_2.0 | all-reduce | flops 2408 | bytes 19264 | tf_op jit(solution)/shard_map/psum | solution.py:40
  78.8 0.2 fusion.4
  79.0 1.5 %copy.37 = bf16[8,300,128]{2,0,1:T(8,128)(2,1)} copy(bf16[8,300,128]{1,0,2:T(8,128)(2,1)S(1)} %fusion.4) | data formatting | bytes 1228800
  80.5 0.7 broadcast_divide_fusion
  (9 shorter events, 0.2 us)
Async XLA Ops:
  0.6 22.2 %copy-start = (f32[24,24]{1,0:T(8,128)S(1)}, f32[24,24]{1,0:T(8,128)}, u32[]{:S(2)}) copy-start(f32[24,24]{1,0:T(8,128)} %param.9) | copy-start | bytes 6916
  2.2 11.2 %collective-permute-start = (bf16[3,300,64]{1,0,2:T(4,128)(2,1)S(1)}, bf16[3,300,64]{1,0,2:T(4,128)(2,1)S(1)}, u32[]{:S(2)}, u32[]{:S(2)}) collective-permute-start(bf16[3,300,64]{1,0,2:T(4,128)(2,1)S(1)} %slice.20), channel_id=1, source_target_pairs={{0,30},{2,0},{4,2},{6,4},{8,6},{10,8},{12,10},{14,12},{16,14},{18,... | collective-permute-start | bytes 345608 | tf_op jit(solution)/shard_map/ppermute | solution.py:10
  15.5 7.4 %copy-start.1 = (f32[128]{0:T(128)S(1)}, f32[128]{0:T(128)}, u32[]{:S(2)}) copy-start(f32[128]{0:T(128)} %param.8) | copy-start | bytes 1540
where the time goes:
time: 81.4 us; the launch traced here: 81.1 us
  blocking collectives  42.6 us (52%)
  local copies, waits for them, and re-layouts  20.2 us (25%)
  starting transfers between devices  7.01 us (9%)
  matrix products  4.58 us (6%)
  other arithmetic  4.38 us (5%)
  waiting for transfers between devices  1.51 us (2%)
    psum x1, blocking collectives, local(): norm_sums, force_sums = lax.psum((norm_sums, force_sums), ('elem', 'param'))  40.7 us
    gather x1, local copies, waits for them, and re-layouts, local(): element_basis = extended[:, :, corner_ids]  9.92 us
    ppermute x1, starting transfers between devices, passed_along(): lax.ppermute(value, axis, [(i, (i + by) % peers) for i in range(peers)])  7.01 us
    gather x2, local copies, waits for them, and re-layouts, local(): displaced[:, :, corner_ids].reshape(snaps, 24, elem_count)  4.05 us
    dot_general x1, matrix products, local(): jnp.einsum('cmae,scae->sme', element_basis, forces, preferred_element_typ...  3.98 us
    unnamed x7, local copies, waits for them, and re-layouts  2.95 us
    concatenate x2, other arithmetic, local(): extended = jnp.concatenate([basis_rows, ghost_rows], axis=2)  2.76 us
    slice x3, local copies, waits for them, and re-layouts, local(): extended[component]  2.6 us
  transfers between devices with their start and end apart: 1, of which 1 were waited for; matrix products, arithmetic and copies ran while one was open for 1% of the time, Pallas kernels for 0%

commit v1 on v0

--- a/solution.py
+++ b/solution.py
@@ -3,6 +3,10 @@
 import jax.numpy as jnp
 from jax import lax
 from jax.sharding import PartitionSpec as P
+
+connect_sites = lambda panel, axis_name, group_axis: jax.lax.psum(
+    jax.lax.psum(panel, axis_name=axis_name), axis_name=group_axis
+)
 
 
 def passed_along(value, axis, by):
@@ -37,7 +41,7 @@
     matrix = jnp.einsum("cmae,scae->sme", element_basis, forces, preferred_element_type=jnp.float32)
     norm_sums = jnp.sum(jnp.sqrt(jnp.sum(matrix * matrix, axis=1)), axis=1)
     force_sums = jnp.sum(matrix, axis=2)
-    norm_sums, force_sums = lax.psum((norm_sums, force_sums), ("elem", "param"))
+    norm_sums, force_sums = connect_sites((norm_sums, force_sums), "param", "elem")
     elem_total = elem_count * lax.axis_size("elem") * cycle_size
     row_scale = norm_sums / elem_total
     target = force_sums / (row_scale[:, None] * math.sqrt(elem_total))

time: 81.4 us -> 122 us (1.50)
  blocking collectives: 42.6 us -> 82.9 us
    psum x1 -> x2, blocking collectives: 40.7 us -> 81 us  [the longest x1 77.7 us: jax.lax.psum(jax.lax.psum(panel, axis_name=axis_name), axis_name=group_axis)]
where the time goes in v1:
time: 122 us; the launch traced here: 121 us
  blocking collectives  82.9 us (68%)
  local copies, waits for them, and re-layouts  20.2 us (17%)
  starting transfers between devices  7.01 us (6%)
  matrix products  4.58 us (4%)
  other arithmetic  4.38 us (4%)
  waiting for transfers between devices  1.51 us (1%)
    psum x1, blocking collectives, jax.lax.psum(jax.lax.psum(panel, axis_name=axis_name), axis_name=group_axis)  77.7 us
    gather x1, local copies, waits for them, and re-layouts, local(): element_basis = extended[:, :, corner_ids]  9.92 us
    ppermute x1, starting transfers between devices, passed_along(): lax.ppermute(value, axis, [(i, (i + by) % peers) for i in range(peers)])  7.01 us
    gather x2, local copies, waits for them, and re-layouts, local(): displaced[:, :, corner_ids].reshape(snaps, 24, elem_count)  4.05 us
    dot_general x1, matrix products, local(): jnp.einsum('cmae,scae->sme', element_basis, forces, preferred_element_typ...  3.98 us
    psum x1, blocking collectives, jax.lax.psum(panel, axis_name=axis_name)  3.29 us
    unnamed x7, local copies, waits for them, and re-layouts  2.95 us
    concatenate x2, other arithmetic, local(): extended = jnp.concatenate([basis_rows, ghost_rows], axis=2)  2.76 us
  transfers between devices with their start and end apart: 1, of which 1 were waited for; matrix products, arithmetic and copies ran while one was open for 1% of the time, Pallas kernels for 0%

profile of v1, /device:TPU:0, one launch (start us, length us, event | category | flops | bytes accessed | tf_op | source)
XLA Modules:
  0.0 121.4 jit_solution(5834596987355721556)
XLA Ops:
  0.6 1.5 %copy.29 = bf16[3,300,256]{1,0,2:T(4,128)(2,1)S(1)} copy(bf16[3,300,256]{2,1,0:T(8,128)(2,1)} %param.6) | data formatting | bytes 921600 | tf_op args[1]
  2.2 7.0 %collective-permute-start = (bf16[3,300,64]{1,0,2:T(4,128)(2,1)S(1)}, bf16[3,300,64]{1,0,2:T(4,128)(2,1)S(1)}, u32[]{:S(2)}, u32[]{:S(2)}) collective-permute-start(bf16[3,300,64]{1,0,2:T(4,128)(2,1)S(1)} %slice.20), channel_id=1, source_target_pairs={{0,30},{2,0},{4,2},{6,4},{8,6},{10,8},{12,10},{14,12},{16,14},{18,... | collective-permute-start | bytes 345608 | tf_op jit(solution)/shard_map/ppermute | solution.py:14
  9.2 1.9 %all-gather = bf16[2,4,300]{2,1,0:T(4,128)(2,1)S(1)} all-gather(bf16[1,4,300]{2,1,0:T(4,128)(2,1)} %bitcast.72), channel_id=1, replica_groups=mesh['elem'=16,'param'=2] {'param'}, dimensions={0}, use_global_device_ids=true | all-gather | bytes 7200 | tf_op jit(solution)/shard_map/all_gather | solution.py:26
  11.2 0.7 fusion.21
  11.9 1.5 %collective-permute-done = bf16[3,300,64]{1,0,2:T(4,128)(2,1)S(1)} collective-permute-done((bf16[3,300,64]{1,0,2:T(4,128)(2,1)S(1)}, bf16[3,300,64]{1,0,2:T(4,128)(2,1)S(1)}, u32[]{:S(2)}, u32[]{:S(2)}) %collective-permute-start) | collective-permute-done | bytes 115232 | tf_op jit(solution)/shard_map/ppermute | solution.py:14
  13.4 2.1 %fusion.12 = (bf16[1,300,320]{1,0,2:T(2,128)(2,1)S(1)}, bf16[1,300,320]{1,0,2:T(2,128)(2,1)S(1)}, bf16[1,300,320]{1,0,2:T(2,128)(2,1)S(1)}) fusion(bf16[3,300,256]{1,0,2:T(4,128)(2,1)S(1)} %copy.29, bf16[3,300,64]{1,0,2:T(4,128)(2,1)S(1)} %collective-permute-done), kind=kLoop, calls=%fused_computation.28 | loop fusion | flops 288000 | bytes 1152000 | tf_op jit(solution)/shard_map/concatenate | solution.py:21
  15.5 0.9 copy.30
  16.3 0.9 copy.31
  17.4 0.2 fusion.10
  17.5 0.9 copy.32
  18.4 0.1 fusion.11
  18.5 0.2 copy.33
  18.8 3.6 %gather_fusion = bf16[1024,8,3]{1,2,0:T(4,128)(2,1)S(1)} fusion(bf16[8,3,320]{0,1,2:T(4,128)(2,1)S(1)} %copy.33, s32[1024]{0:T(1024)S(1)} %fusion.21), kind=kCustom, calls=%fused_computation | custom fusion | bytes 102400 | tf_op jit(solution)/shard_map/gather | solution.py:35
  22.3 0.5 copy.34
  22.9 0.2 fusion.8
  23.0 0.4 copy.36
  23.5 0.7 pad_maximum_fusion
  24.1 9.9 %gather_fusion.1 = bf16[1024,3,300]{2,1,0:T(4,128)(2,1)} fusion(bf16[3,300,320]{1,0,2:T(4,128)(2,1)S(1)} %pad_maximum_fusion, s32[1024]{0:T(1024)S(1)} %fusion.21), kind=kCustom, calls=%fused_computation.1 | custom fusion | bytes 3690496 | tf_op jit(solution)/shard_map/gather | solution.py:24
  34.1 4.0 %bitcast_reduce_fusion = (f32[8,300]{1,0:T(8,128)S(1)}, f32[8,128]{0,1:T(8,128)S(1)}, f32[128,8,300,1]{2,1,3,0:T(8,128)S(1)}) fusion(bf16[8,3,8,128]{2,0,1,3:T(8,128)(2,1)S(1)} %copy.36, bf16[8,128,3,300]{3,2,1,0:T(4,128)(2,1)} %bitcast.71), kind=kOutput, calls=%fused_computation.5 | convolution fusion | flops 15663776 | bytes 3134848 | tf_op jit(solution)/shard_map/cmae,scae->sme/dot_general | solution.py:41
  38.1 3.3 %all-reduce.1 = (f32[8]{0:T(128)S(1)}, f32[8,300]{1,0:T(8,128)S(1)}) all-reduce(f32[8]{0:T(128)S(1)} %sqrt_reduce_fusion, f32[8,300]{1,0:T(8,128)S(1)} %get-tuple-element.10), channel_id=1, replica_groups=mesh['elem'=16,'param'=2] {'param'}, use_global_device_ids=true, to_apply=%region_2.0 | all-reduce | flops 2408 | bytes 19264 | tf_op jit(solution)/shard_map/psum | solution.py:8
  41.4 77.7 %all-reduce = (f32[8]{0:T(128)S(1)}, f32[8,300]{1,0:T(8,128)S(1)}) all-reduce(f32[8]{0:T(128)S(1)} %get-tuple-element.14, f32[8,300]{1,0:T(8,128)S(1)} %get-tuple-element.15), channel_id=1, replica_groups=mesh['elem'=16,'param'=2] {'elem'}, use_global_device_ids=true, to_apply=%region_3.0 | all-reduce | flops 2408 | bytes 19264 | tf_op jit(solution)/shard_map/psum | solution.py:7
  119.1 0.2 fusion.4
  119.3 1.5 %copy.37 = bf16[8,300,128]{2,0,1:T(8,128)(2,1)} copy(bf16[8,300,128]{1,0,2:T(8,128)(2,1)S(1)} %fusion.4) | data formatting | bytes 1228800
  120.7 0.7 broadcast_divide_fusion
  (10 shorter events, 0.3 us)
Async XLA Ops:
  0.6 22.2 %copy-start = (f32[24,24]{1,0:T(8,128)S(1)}, f32[24,24]{1,0:T(8,128)}, u32[]{:S(2)}) copy-start(f32[24,24]{1,0:T(8,128)} %param.9) | copy-start | bytes 6916
  2.2 11.2 %collective-permute-start = (bf16[3,300,64]{1,0,2:T(4,128)(2,1)S(1)}, bf16[3,300,64]{1,0,2:T(4,128)(2,1)S(1)}, u32[]{:S(2)}, u32[]{:S(2)}) collective-permute-start(bf16[3,300,64]{1,0,2:T(4,128)(2,1)S(1)} %slice.20), channel_id=1, source_target_pairs={{0,30},{2,0},{4,2},{6,4},{8,6},{10,8},{12,10},{14,12},{16,14},{18,... | collective-permute-start | bytes 345608 | tf_op jit(solution)/shard_map/ppermute | solution.py:14
  15.5 7.4 %copy-start.1 = (f32[128]{0:T(128)S(1)}, f32[128]{0:T(128)}, u32[]{:S(2)}) copy-start(f32[128]{0:T(128)} %param.8) | copy-start | bytes 1540
